TPU v7x, 512 devices: a whole 4x4x16 slice. The times are simulated.
512 devices in a mesh: query: 4 (over x), cand: 32 (over z_hi, y, core), tensor: 4 (over z_lo).
Axes of the slice: x: 4, y: 4, z: 16 (z_hi: 4, z_lo: 4; z = z_hi * 4 + z_lo), core: 2. Of those that a mesh axis runs over, the one named last changes fastest.
Arguments:
- cand_states: bfloat16 [131072, 2048], P(('query', 'cand'), 'tensor'), parts along dimension 0, may hold values from -6 to 6
- prefix_states: bfloat16 [256, 2048], P(('query', 'cand'), 'tensor'), parts along dimension 0, may hold values from -6 to 6
- norm_gain: float32 [2048], replicated, may hold values from 0.5 to 1.5
- w_query: bfloat16 [2048, 1024], P(None, 'tensor'), may hold values from -1 to 1
- w_key: bfloat16 [2048, 256], P(None, 'tensor'), may hold values from -1 to 1
- w_value: bfloat16 [2048, 256], P(None, 'tensor'), may hold values from -0.125 to 0.125
- w_out: bfloat16 [1024, 2048], P('tensor'), may hold values from -1.5 to 1.5
- cand_lengths: int32 [1024], P(('query', 'cand')), parts along dimension 0, may hold values from 32 to 128, as said below
Outputs:
- attn_out: bfloat16 [131072, 2048], P(('query', 'cand', 'tensor')), parts along dimension 0
There are 4 independent parts, one for each index of `query`. A program takes and returns all parts, laid end to end along the dimension named above; an argument that names none is the same for every part. Nothing has to cross between parts.
Inputs may be any that keep to these rules, and one draw needn't show every extreme that they name: `cand_lengths`: some candidate has all 128 slots live.
All inputs are finite; a program needn't handle non-finite values.
Results may differ from a plain program's by a relative error of at most 0.013.
Values may be sent and summed in bfloat16 or wider, within the bound.
A program may use at most 64 MiB of HBM per device.

v0:
```python
import jax
import jax.numpy as jnp
from jax import lax
from jax.sharding import PartitionSpec as P

epsilon = 1e-06
theta_base = 10000.0


def in_one_piece(arrays, axis, dim, along):
    both = jnp.concatenate(arrays, axis=along)
    filled, at, outs = (lax.all_gather(both, axis, axis=dim, tiled=True), 0, [])
    for a in arrays:
        outs.append(lax.slice_in_dim(filled, at, at + a.shape[along], axis=along))
        at += a.shape[along]
    return tuple(outs)


def joined_along(tiles, dim):
    lengths = list(tiles.shape[1:])
    lengths[dim] *= tiles.shape[0]
    return jnp.moveaxis(tiles, 0, dim).reshape(lengths)


def from_everyone(value, axis):
    copies = jnp.broadcast_to(value, (lax.axis_size(axis), *value.shape))
    return lax.all_to_all(copies, axis, split_axis=0, concat_axis=0, tiled=True)


def collect(value, axis, dim):
    return joined_along(from_everyone(value, axis), dim)


def in_one_piece_2(arrays, axis, dim, along):
    ends, at = ([], 0)
    for a in arrays[:-1]:
        at += a.shape[along]
        ends.append(at)
    both = jnp.concatenate(arrays, axis=along)
    return tuple(jnp.split(collect(both, axis, dim), ends, axis=along))


def rotate(values, positions):
    half_size = values.shape[-1] // 2
    frequency = theta_base ** (-jnp.arange(half_size, dtype=jnp.float32) * 2.0 / values.shape[-1])
    angles = positions.astype(jnp.float32)[:, None] * frequency[None, :]
    cosine = jnp.cos(angles)
    sine_part = jnp.sin(angles)
    lower_half = values[:, :half_size]
    upper_half = values[:, half_size:]
    return jnp.concatenate(
        [
            lower_half * cosine - upper_half * sine_part,
            upper_half * cosine + lower_half * sine_part,
        ],
        axis=-1,
    )


def normalize(states, norm_gain):
    values = states.astype(jnp.float32)
    square = jnp.mean(values * values, axis=-1, keepdims=True)
    return (values * lax.rsqrt(square + epsilon) * norm_gain[None, :]).astype(jnp.bfloat16)


def self_scores_of(queries, cand_keys):
    scores = jnp.einsum("cqd,ckd->cqk", queries, cand_keys, preferred_element_type=jnp.float32)
    slots = jnp.arange(scores.shape[1], dtype=jnp.int32)
    causal = slots[:, None] >= slots[None, :]
    return jnp.where(causal[None], scores, -jnp.inf)


def body(cand_states, prefix_states, norm_gain, w_query, w_key, w_value, w_out, cand_lengths):
    cand_full, prefix_full = in_one_piece((cand_states, prefix_states), "tensor", 1, 0)
    normed_cand = normalize(cand_full, norm_gain)
    normed_prefix = normalize(prefix_full, norm_gain)
    cand_count = cand_lengths.shape[0]
    cand_len = cand_full.shape[0] // cand_count
    prefix_rows = prefix_full.shape[0]
    cand_groups = lax.axis_size("cand")
    tensor_size = lax.axis_size("tensor")
    prefix_len = prefix_rows * cand_groups
    head_size = w_query.shape[1]
    cand_pos = prefix_len + jnp.tile(jnp.arange(cand_len, dtype=jnp.int32), cand_count)
    cand_key = jnp.dot(normed_cand, w_key, preferred_element_type=jnp.float32).astype(jnp.bfloat16)
    cand_value = jnp.dot(normed_cand, w_value, preferred_element_type=jnp.float32).astype(
        jnp.bfloat16
    )
    prefix_key = jnp.dot(normed_prefix, w_key, preferred_element_type=jnp.float32).astype(
        jnp.bfloat16
    )
    prefix_value = jnp.dot(normed_prefix, w_value, preferred_element_type=jnp.float32).astype(
        jnp.bfloat16
    )
    query_rows = rotate(
        jnp.dot(normed_cand, w_query, preferred_element_type=jnp.float32), cand_pos
    ) * head_size ** (-0.5)
    queries = query_rows.astype(jnp.bfloat16).reshape(cand_count, cand_len, head_size)
    cand_key, cand_value, prefix_key, prefix_value = in_one_piece_2(
        (cand_key, cand_value, prefix_key, prefix_value), "tensor", 1, 0
    )
    prefix_pos = lax.axis_index("cand") * prefix_rows + jnp.arange(prefix_rows, dtype=jnp.int32)
    prefix_key = rotate(prefix_key.astype(jnp.float32), prefix_pos).astype(jnp.bfloat16)
    cand_keys = (
        rotate(cand_key.astype(jnp.float32), cand_pos)
        .astype(jnp.bfloat16)
        .reshape(cand_count, cand_len, head_size)
    )
    cand_values = cand_value.reshape(cand_count, cand_len, head_size)
    self_scores = self_scores_of(queries, cand_keys)
    highest = self_scores.max(-1)
    weights = jnp.exp(self_scores - highest[..., None])
    highest, divisor, summed = (
        highest,
        weights.sum(-1),
        jnp.einsum(
            "cqk,ckd->cqd",
            weights.astype(jnp.bfloat16),
            cand_values,
            preferred_element_type=jnp.float32,
        ),
    )
    key_piece, value_piece = in_one_piece((prefix_key, prefix_value), "cand", 0, 1)
    prefix_scores = jnp.einsum(
        "cqd,kd->cqk", queries, key_piece, preferred_element_type=jnp.float32
    )
    new_highest = jnp.maximum(highest, prefix_scores.max(-1))
    rescale = jnp.exp(highest - new_highest)
    weights = jnp.exp(prefix_scores - new_highest[..., None])
    divisor = divisor * rescale + weights.sum(-1)
    summed = summed * rescale[..., None] + jnp.einsum(
        "cqk,kd->cqd", weights.astype(jnp.bfloat16), value_piece, preferred_element_type=jnp.float32
    )
    highest, divisor, summed = (new_highest, divisor, summed)
    slots = jnp.arange(cand_len, dtype=jnp.int32)
    live_rows = slots[None, :] < cand_lengths[:, None]
    head_rows = jnp.where(live_rows[..., None], summed / divisor[..., None], 0.0)
    head_rows = head_rows.reshape(cand_count * cand_len, head_size).astype(jnp.bfloat16)
    row_count = head_rows.shape[0] // tensor_size
    all_heads = lax.all_to_all(head_rows, "tensor", split_axis=0, concat_axis=1, tiled=True)
    full_out = lax.all_gather(w_out, "tensor", axis=0, tiled=True)
    summed_out = jnp.zeros((row_count, full_out.shape[1]), jnp.float32)
    for head_index in range(tensor_size):
        head_term = jnp.dot(
            all_heads[:, head_index * head_size : (head_index + 1) * head_size],
            full_out[head_index * head_size : (head_index + 1) * head_size],
            preferred_element_type=jnp.float32,
        )
        summed_out = summed_out + lax.optimization_barrier(head_term.astype(jnp.bfloat16)).astype(
            jnp.float32
        )
    return summed_out.astype(jnp.bfloat16)


def solution(mesh):
    in_specs = (
        P(("query", "cand"), "tensor"),
        P(("query", "cand"), "tensor"),
        P(),
        P(None, "tensor"),
        P(None, "tensor"),
        P(None, "tensor"),
        P("tensor", None),
        P(("query", "cand")),
    )
    out_specs = P(("query", "cand", "tensor"), None)
    return jax.shard_map(body, mesh=mesh, in_specs=in_specs, out_specs=out_specs, check_vma=False)
```

profile of v0, /device:TPU:1, one launch (start us, length us, event | category | flops | bytes accessed | tf_op | source)
XLA Modules:
  0.0 256.7 jit_solution(11628794614377574297)
XLA Ops:
  6.5 2.4 pad_maximum_fusion
  8.9 95.2 %all-gather.4.cloned.1.call-done = bf16[1026,2048]{1,0:T(8,128)(2,1)} async-done(((bf16[1026,512]{1,0:T(8,128)(2,1)}), bf16[1026,2048]{1,0:T(8,128)(2,1)}) %all-gather.4.cloned.1.call-update) | async-done | bytes 4202512 | tf_op jit(solution)/shard_map/all_gather | solution.py:12
  104.2 3.1 %fusion = f32[1024]{0:T(1024)S(1)} fusion(bf16[1026,2048]{1,0:T(8,128)(2,1)} %all-gather.4.cloned.1.call-done), kind=kLoop, calls=%fused_computation.2 | loop fusion | flops 6290432 | bytes 4198400 | tf_op jit(solution)/shard_map/reduce_sum | solution.py:62
  107.3 2.9 %fusion.2 = bf16[1024,2048]{1,0:T(8,128)(2,1)S(1)} fusion(f32[2048]{0:T(1024)S(1)} %copy-done.5, f32[1024]{0:T(1024)S(1)} %add_rsqrt_fusion, bf16[1026,2048]{1,0:T(8,128)(2,1)} %all-gather.4.cloned.1.call-done), kind=kLoop, calls=%fused_computation.4 | loop fusion | flops 8388608 | bytes 8400896 | tf_op jit(solution)/shard_map/convert_element_type | solution.py:63
  110.2 1.4 convolution_convert_fusion.4
  111.6 1.4 convolution_convert_fusion.5
  113.0 0.9 fusion.42
  113.9 1.0 convolution_convert_fusion.7
  115.0 1.0 convolution_convert_fusion.6
  116.3 1.2 broadcast_in_dim.24
  117.4 3.5 %all-to-all-start = ((bf16[4,2052,64]{1,2,0:T(8,128)(2,1)}), bf16[4,2052,64]{1,2,0:T(8,128)(2,1)S(1)}, u32[]{:S(2)}, u32[]{:S(2)}) async-start(bf16[4,2052,64]{1,2,0:T(8,128)(2,1)} %broadcast_in_dim.24), calls=%async_computation | async-start | bytes 2228224 | tf_op jit(solution)/shard_map/all_to_all | solution.py:27
  121.0 0.7 all-gather.6.cloned.1.call-update
  121.9 4.4 %fusion.68 = f32[1024,256]{1,0:T(8,128)} fusion(bf16[1024,2048]{1,0:T(8,128)(2,1)} %copy-done.1, bf16[2048,256]{1,0:T(8,128)(2,1)S(1)} %copy-done), kind=kOutput, calls=%fused_computation.100 | convolution fusion | flops 1073741824 | bytes 6291456 | tf_op jit(solution)/shard_map/dot_general | solution.py:96
  126.3 21.3 %all-to-all-done = bf16[4,2052,64]{1,2,0:T(8,128)(2,1)S(1)} async-done(((bf16[4,2052,64]{1,2,0:T(8,128)(2,1)}), bf16[4,2052,64]{1,2,0:T(8,128)(2,1)S(1)}, u32[]{:S(2)}, u32[]{:S(2)}) %all-to-all-start) | async-done | bytes 1050656 | tf_op jit(solution)/shard_map/all_to_all | solution.py:27
  147.6 1.0 fusion.62
  148.7 0.9 fusion.64
  149.8 1.2 copy.45
  151.6 65.6 %all-gather = bf16[32,2,512]{2,1,0:T(2,128)(2,1)S(1)} all-gather(bf16[1,2,512]{2,1,0:T(2,128)(2,1)S(1)} %maximum_bitcast_fusion), channel_id=1, replica_groups=mesh['query'=4,'cand'=32,'tensor'=4] {'cand'}, dimensions={0}, use_global_device_ids=true | all-gather | bytes 67584 | tf_op jit(solution)/shard_map/all_gather | solution.py:12
  217.2 1.1 copy.48
  218.4 3.8 %fusion.22 = (bf16[1024,128]{1,0:T(8,128)(2,1)S(1)}, bf16[1024,128]{1,0:T(8,128)(2,1)S(1)}, f32[1024,128]{1,0:T(8,128)S(1)}, f32[1024,128]{1,0:T(8,128)S(1)}) fusion(f32[1024,128]{1,0:T(8,128)S(1)} %copy.45, f32[1024,128]{1,0:T(8,128)S(1)} %copy.44, f32[128]{0:T(128)S(1)} %multiply_power_fusion, f32[1024]{0:T(1024)S(1)} %convert_bitcast_fusion, ...), kind=kLoop, calls=%fused_computation.40 | loop fusion | flops 1966080 | bytes 3674624 | tf_op jit(solution)/shard_map/convert.7
  222.2 0.3 fusion.67
  222.5 0.3 fusion.66
  223.0 0.4 convolution_multiply_fusion
  223.4 0.4 fusion.5
  223.8 1.0 copy.42
  224.8 4.7 %all-to-all-start.1 = ((bf16[4,256,256]{1,2,0:T(8,128)(2,1)}), bf16[4,256,256]{1,2,0:T(8,128)(2,1)S(1)}, u32[]{:S(2)}, u32[]{:S(2)}) async-start(bf16[4,256,256]{1,2,0:T(8,128)(2,1)} %copy.42), calls=%async_computation.1 | async-start | bytes 1048576 | tf_op jit(solution)/shard_map/all_to_all | solution.py:140
  229.5 14.1 %all-to-all-done.1 = bf16[4,256,256]{1,2,0:T(8,128)(2,1)S(1)} async-done(((bf16[4,256,256]{1,2,0:T(8,128)(2,1)}), bf16[4,256,256]{1,2,0:T(8,128)(2,1)S(1)}, u32[]{:S(2)}, u32[]{:S(2)}) %all-to-all-start.1) | async-done | bytes 524320 | tf_op jit(solution)/shard_map/all_to_all | solution.py:140
  243.7 1.8 convolution_convert_fusion.3
  245.5 1.7 convolution_convert_fusion.2
  247.2 0.5 convolution_convert_fusion.1
  247.7 0.5 convolution_convert_fusion
  248.1 1.7 add_convert_fusion
  (43 shorter events, 1.6 us)
Async XLA Ops:
  6.5 115.3 %copy-start = (bf16[2048,256]{1,0:T(8,128)(2,1)S(1)}, bf16[2048,256]{1,0:T(8,128)(2,1)}, u32[]{:S(2)}) copy-start(bf16[2048,256]{1,0:T(8,128)(2,1)} %param.11) | copy-start | bytes 3145732
  6.5 100.7 %copy-start.5 = (f32[2048]{0:T(1024)S(1)}, f32[2048]{0:T(1024)}, u32[]{:S(2)}) copy-start(f32[2048]{0:T(1024)} %param.10) | copy-start | bytes 24580
  6.5 97.6 %all-gather.4.cloned.1.call-start = ((), (), s32[]{:S(2)}) async-start(), calls=%async_computation.2 | async-start | bytes 5283840 | tf_op jit(solution)/shard_map/all_gather | solution.py:12
  107.3 2.9 %copy-start.4 = (bf16[2048,64]{0,1:T(8,128)(2,1)S(1)}, bf16[2048,64]{0,1:T(8,128)(2,1)}, u32[]{:S(2)}) copy-start(bf16[2048,64]{0,1:T(8,128)(2,1)} %param.13) | copy-start | bytes 786436
  110.2 2.8 %copy-start.1 = (bf16[1024,2048]{1,0:T(8,128)(2,1)}, bf16[1024,2048]{1,0:T(8,128)(2,1)S(1)}, u32[]{:S(2)}) copy-start(bf16[1024,2048]{1,0:T(8,128)(2,1)S(1)} %fusion.2) | copy-start | bytes 12582916
  110.2 1.4 copy-start.3
  113.0 8.8 %copy-start.6 = (s32[8]{0:T(128)S(1)}, s32[8]{0:T(128)}, u32[]{:S(2)}) copy-start(s32[8]{0:T(128)} %param.15) | copy-start | bytes 100
  117.4 30.2 %all-to-all-start = ((bf16[4,2052,64]{1,2,0:T(8,128)(2,1)}), bf16[4,2052,64]{1,2,0:T(8,128)(2,1)S(1)}, u32[]{:S(2)}, u32[]{:S(2)}) async-start(bf16[4,2052,64]{1,2,0:T(8,128)(2,1)} %broadcast_in_dim.24), calls=%async_computation | async-start | bytes 2228224 | tf_op jit(solution)/shard_map/all_to_all | solution.py:27
  121.0 108.6 %all-gather.6.cloned.1.call-start = ((), (), s32[]{:S(2)}) async-start(), calls=%async_computation.3 | async-start | bytes 5242880 | tf_op jit(solution)/shard_map/all_gather | solution.py:141
  224.8 18.9 %all-to-all-start.1 = ((bf16[4,256,256]{1,2,0:T(8,128)(2,1)}), bf16[4,256,256]{1,2,0:T(8,128)(2,1)S(1)}, u32[]{:S(2)}, u32[]{:S(2)}) async-start(bf16[4,256,256]{1,2,0:T(8,128)(2,1)} %copy.42), calls=%async_computation.1 | async-start | bytes 1048576 | tf_op jit(solution)/shard_map/all_to_all | solution.py:140
  243.7 3.5 %copy-start.2 = (bf16[1024,2048]{1,0:T(8,128)(2,1)S(1)}, bf16[1024,2048]{1,0:T(8,128)(2,1)}, u32[]{:S(2)}) copy-start(bf16[1024,2048]{1,0:T(8,128)(2,1)} %all-gather.6.cloned.1.call-done) | copy-start | bytes 12582916
Sparse Core Ops, SparseCore 0:
  9.4 94.6 all-gather.3
  123.9 93.5 all-gather.5
where the time goes:
time: 257 us
  waiting for transfers between devices  131 us (51%)
  blocking collectives  65.6 us (26%)
  other arithmetic  15.3 us (6%)
  matrix products  15 us (6%)
  between operations  13.7 us (5%)
  starting transfers between devices  8.3 us (3%)
  local copies, waits for them, and re-layouts  7.31 us (3%)
    all_gather x1, waiting for transfers between devices, in_one_piece(): filled, at, outs = (lax.all_gather(both, axis, axis=dim, tiled=True), 0, [])  95.2 us
    all_gather x1, blocking collectives, in_one_piece(): filled, at, outs = (lax.all_gather(both, axis, axis=dim, tiled=True), 0, [])  65.6 us
    all_to_all x1, waiting for transfers between devices, from_everyone(): return lax.all_to_all(copies, axis, split_axis=0, concat_axis=0, tiled=True)  21.3 us
    all_to_all x1, waiting for transfers between devices, body(): lax.all_to_all(head_rows, 'tensor', split_axis=0, concat_axis=1, tiled=True)  14.1 us
  transfers between devices with their start and end apart: 4, of which 3 were waited for; matrix products, arithmetic and copies ran while one was open for 6% of the time, Pallas kernels for 0%

commit v1 on v0

--- a/solution.py
+++ b/solution.py
@@ -137,7 +137,12 @@
     head_rows = jnp.where(live_rows[..., None], summed / divisor[..., None], 0.0)
     head_rows = head_rows.reshape(cand_count * cand_len, head_size).astype(jnp.bfloat16)
     row_count = head_rows.shape[0] // tensor_size
-    all_heads = lax.all_to_all(head_rows, "tensor", split_axis=0, concat_axis=1, tiled=True)
+    all_heads = jnp.concatenate(
+        lax.all_to_all(
+            jnp.stack(jnp.split(head_rows, lax.axis_size("tensor"), axis=0)), "tensor", 0, 0
+        ),
+        axis=1,
+    )
     full_out = lax.all_gather(w_out, "tensor", axis=0, tiled=True)
     summed_out = jnp.zeros((row_count, full_out.shape[1]), jnp.float32)
     for head_index in range(tensor_size):

time: 257 us -> 258 us (level)
  no operation moved by 1% of the time
where the time goes in v1:
time: 258 us; the launch traced here: 257 us
  waiting for transfers between devices  131 us (51%)
  blocking collectives  65.6 us (25%)
  other arithmetic  16.2 us (6%)
  matrix products  15 us (6%)
  between operations  13.8 us (5%)
  starting transfers between devices  8.3 us (3%)
  local copies, waits for them, and re-layouts  6.74 us (3%)
    all_gather x1, waiting for transfers between devices, in_one_piece(): filled, at, outs = (lax.all_gather(both, axis, axis=dim, tiled=True), 0, [])  95.2 us
    all_gather x1, blocking collectives, in_one_piece(): filled, at, outs = (lax.all_gather(both, axis, axis=dim, tiled=True), 0, [])  65.6 us
    all_to_all x1, waiting for transfers between devices, from_everyone(): return lax.all_to_all(copies, axis, split_axis=0, concat_axis=0, tiled=True)  21.3 us
    all_to_all x1, waiting for transfers between devices, body(): lax.all_to_all(jnp.stack(jnp.split(head_rows, lax.axis_size('tensor'), ax...  14.1 us
  transfers between devices with their start and end apart: 4, of which 3 were waited for; matrix products, arithmetic and copies ran while one was open for 6% of the time, Pallas kernels for 0%

profile of v1, /device:TPU:1, one launch (start us, length us, event | category | flops | bytes accessed | tf_op | source)
XLA Modules:
  0.0 257.0 jit_solution(9171372898754829038)
XLA Ops:
  6.5 2.4 pad_maximum_fusion
  8.9 95.2 %all-gather.4.cloned.1.call-done = bf16[1026,2048]{1,0:T(8,128)(2,1)} async-done(((bf16[1026,512]{1,0:T(8,128)(2,1)}), bf16[1026,2048]{1,0:T(8,128)(2,1)}) %all-gather.4.cloned.1.call-update) | async-done | bytes 4202512 | tf_op jit(solution)/shard_map/all_gather | solution.py:12
  104.2 3.1 %fusion = f32[1024]{0:T(1024)S(1)} fusion(bf16[1026,2048]{1,0:T(8,128)(2,1)} %all-gather.4.cloned.1.call-done), kind=kLoop, calls=%fused_computation.2 | loop fusion | flops 6290432 | bytes 4198400 | tf_op jit(solution)/shard_map/reduce_sum | solution.py:62
  107.3 2.9 %fusion.2 = bf16[1024,2048]{1,0:T(8,128)(2,1)S(1)} fusion(f32[2048]{0:T(1024)S(1)} %copy-done.5, f32[1024]{0:T(1024)S(1)} %add_rsqrt_fusion, bf16[1026,2048]{1,0:T(8,128)(2,1)} %all-gather.4.cloned.1.call-done), kind=kLoop, calls=%fused_computation.4 | loop fusion | flops 8388608 | bytes 8400896 | tf_op jit(solution)/shard_map/convert_element_type | solution.py:63
  110.2 1.4 convolution_convert_fusion.4
  111.6 1.4 convolution_convert_fusion.5
  113.0 0.9 fusion.42
  113.9 1.0 convolution_convert_fusion.7
  115.0 1.0 convolution_convert_fusion.6
  116.3 1.2 broadcast_in_dim.24
  117.4 3.5 %all-to-all-start = ((bf16[4,2052,64]{1,2,0:T(8,128)(2,1)}), bf16[4,2052,64]{1,2,0:T(8,128)(2,1)S(1)}, u32[]{:S(2)}, u32[]{:S(2)}) async-start(bf16[4,2052,64]{1,2,0:T(8,128)(2,1)} %broadcast_in_dim.24), calls=%async_computation | async-start | bytes 2228224 | tf_op jit(solution)/shard_map/all_to_all | solution.py:27
  121.0 0.7 all-gather.6.cloned.1.call-update
  121.9 4.4 %fusion.69 = f32[1024,256]{1,0:T(8,128)} fusion(bf16[1024,2048]{1,0:T(8,128)(2,1)} %copy-done.1, bf16[2048,256]{1,0:T(8,128)(2,1)S(1)} %copy-done), kind=kOutput, calls=%fused_computation.102 | convolution fusion | flops 1073741824 | bytes 6291456 | tf_op jit(solution)/shard_map/dot_general | solution.py:96
  126.3 21.3 %all-to-all-done = bf16[4,2052,64]{1,2,0:T(8,128)(2,1)S(1)} async-done(((bf16[4,2052,64]{1,2,0:T(8,128)(2,1)}), bf16[4,2052,64]{1,2,0:T(8,128)(2,1)S(1)}, u32[]{:S(2)}, u32[]{:S(2)}) %all-to-all-start) | async-done | bytes 1050656 | tf_op jit(solution)/shard_map/all_to_all | solution.py:27
  147.6 1.0 fusion.62
  148.7 0.9 fusion.64
  149.8 1.2 copy.54
  151.6 65.6 %all-gather = bf16[32,2,512]{2,1,0:T(2,128)(2,1)S(1)} all-gather(bf16[1,2,512]{2,1,0:T(2,128)(2,1)S(1)} %maximum_bitcast_fusion), channel_id=1, replica_groups=mesh['query'=4,'cand'=32,'tensor'=4] {'cand'}, dimensions={0}, use_global_device_ids=true | all-gather | bytes 67584 | tf_op jit(solution)/shard_map/all_gather | solution.py:12
  217.2 1.1 copy.57
  218.4 3.8 %fusion.22 = (bf16[1024,128]{1,0:T(8,128)(2,1)S(1)}, bf16[1024,128]{1,0:T(8,128)(2,1)S(1)}, f32[1024,128]{1,0:T(8,128)S(1)}, f32[1024,128]{1,0:T(8,128)S(1)}) fusion(f32[1024,128]{1,0:T(8,128)S(1)} %copy.54, f32[1024,128]{1,0:T(8,128)S(1)} %copy.53, f32[128]{0:T(128)S(1)} %multiply_power_fusion, f32[1024]{0:T(1024)S(1)} %convert_bitcast_fusion, ...), kind=kLoop, calls=%fused_computation.40 | loop fusion | flops 1966080 | bytes 3674624 | tf_op jit(solution)/shard_map/convert.7
  222.2 0.3 fusion.68
  222.5 0.3 fusion.67
  223.0 0.4 convolution_multiply_fusion
  223.3 0.4 fusion.5
  224.3 0.9 pad_maximum_fusion.1
  225.1 4.7 %all-to-all-start.1 = ((bf16[4,256,256]{1,2,0:T(8,128)(2,1)}), bf16[4,256,256]{1,2,0:T(8,128)(2,1)S(1)}, u32[]{:S(2)}, u32[]{:S(2)}) async-start(bf16[4,256,256]{1,2,0:T(8,128)(2,1)} %pad_maximum_fusion.1), calls=%async_computation.1 | async-start | bytes 1048576 | tf_op jit(solution)/shard_map/all_to_all | solution.py:141
  229.9 14.1 %all-to-all-done.1 = bf16[4,256,256]{1,2,0:T(8,128)(2,1)S(1)} async-done(((bf16[4,256,256]{1,2,0:T(8,128)(2,1)}), bf16[4,256,256]{1,2,0:T(8,128)(2,1)S(1)}, u32[]{:S(2)}, u32[]{:S(2)}) %all-to-all-start.1) | async-done | bytes 524320 | tf_op jit(solution)/shard_map/all_to_all | solution.py:141
  244.0 1.8 convolution_convert_fusion.3
  245.8 1.7 convolution_convert_fusion.2
  247.5 0.5 convolution_convert_fusion.1
  248.0 0.5 convolution_convert_fusion
  248.5 1.7 add_convert_fusion
  (48 shorter events, 2.0 us)
Async XLA Ops:
  6.5 115.3 %copy-start = (bf16[2048,256]{1,0:T(8,128)(2,1)S(1)}, bf16[2048,256]{1,0:T(8,128)(2,1)}, u32[]{:S(2)}) copy-start(bf16[2048,256]{1,0:T(8,128)(2,1)} %param.11) | copy-start | bytes 3145732
  6.5 100.7 %copy-start.5 = (f32[2048]{0:T(1024)S(1)}, f32[2048]{0:T(1024)}, u32[]{:S(2)}) copy-start(f32[2048]{0:T(1024)} %param.10) | copy-start | bytes 24580
  6.5 97.6 %all-gather.4.cloned.1.call-start = ((), (), s32[]{:S(2)}) async-start(), calls=%async_computation.2 | async-start | bytes 5283840 | tf_op jit(solution)/shard_map/all_gather | solution.py:12
  107.3 2.9 %copy-start.4 = (bf16[2048,64]{0,1:T(8,128)(2,1)S(1)}, bf16[2048,64]{0,1:T(8,128)(2,1)}, u32[]{:S(2)}) copy-start(bf16[2048,64]{0,1:T(8,128)(2,1)} %param.13) | copy-start | bytes 786436
  110.2 2.8 %copy-start.1 = (bf16[1024,2048]{1,0:T(8,128)(2,1)}, bf16[1024,2048]{1,0:T(8,128)(2,1)S(1)}, u32[]{:S(2)}) copy-start(bf16[1024,2048]{1,0:T(8,128)(2,1)S(1)} %fusion.2) | copy-start | bytes 12582916
  110.2 1.4 copy-start.3
  113.0 8.8 %copy-start.6 = (s32[8]{0:T(128)S(1)}, s32[8]{0:T(128)}, u32[]{:S(2)}) copy-start(s32[8]{0:T(128)} %param.15) | copy-start | bytes 100
  117.4 30.2 %all-to-all-start = ((bf16[4,2052,64]{1,2,0:T(8,128)(2,1)}), bf16[4,2052,64]{1,2,0:T(8,128)(2,1)S(1)}, u32[]{:S(2)}, u32[]{:S(2)}) async-start(bf16[4,2052,64]{1,2,0:T(8,128)(2,1)} %broadcast_in_dim.24), calls=%async_computation | async-start | bytes 2228224 | tf_op jit(solution)/shard_map/all_to_all | solution.py:27
  121.0 108.9 %all-gather.6.cloned.1.call-start = ((), (), s32[]{:S(2)}) async-start(), calls=%async_computation.3 | async-start | bytes 5242880 | tf_op jit(solution)/shard_map/all_gather | solution.py:146
  225.1 18.9 %all-to-all-start.1 = ((bf16[4,256,256]{1,2,0:T(8,128)(2,1)}), bf16[4,256,256]{1,2,0:T(8,128)(2,1)S(1)}, u32[]{:S(2)}, u32[]{:S(2)}) async-start(bf16[4,256,256]{1,2,0:T(8,128)(2,1)} %pad_maximum_fusion.1), calls=%async_computation.1 | async-start | bytes 1048576 | tf_op jit(solution)/shard_map/all_to_all | solution.py:141
  244.0 3.5 %copy-start.2 = (bf16[1024,2048]{1,0:T(8,128)(2,1)S(1)}, bf16[1024,2048]{1,0:T(8,128)(2,1)}, u32[]{:S(2)}) copy-start(bf16[1024,2048]{1,0:T(8,128)(2,1)} %all-gather.6.cloned.1.call-done) | copy-start | bytes 12582916
Sparse Core Ops, SparseCore 0:
  9.4 94.6 all-gather.3
  123.9 93.5 all-gather.5
